TPU v7x, 32 devices: a whole 2x2x4 slice. The times are simulated.
32 devices in a mesh: groups: 2 (over y), ctx: 4 (over z), ep: 2 (over x), tp: 2 (over core).
Axes of the slice: x: 2, y: 2, z: 4, core: 2. Of those that a mesh axis runs over, the one named last changes fastest.
Arguments:
- queries: bfloat16 [4, 512, 5120], P(('groups', 'ep'), 'ctx', 'tp'), parts along dimension 0, may hold values from -128 to 128
- keys: bfloat16 [4, 512, 1024], P(('groups', 'ep'), 'ctx', 'tp'), parts along dimension 0, may hold values from -6 to 6
- values: bfloat16 [4, 512, 1024], P(('groups', 'ep'), 'ctx', 'tp'), parts along dimension 0, may hold values from -6 to 6
- expert_ids: int32 [4, 512, 1], P(('groups', 'ep'), 'ctx'), parts along dimension 0, may hold values from 0 to 127, as said below
- router: bfloat16 [5120, 2], P('tp', 'ep'), may hold values from -0.3125 to 0.3125
- w_gate: bfloat16 [2, 5120, 4096], P('ep', 'tp', 'ctx'), may hold values from -0.3125 to 0.3125
- w_up: bfloat16 [2, 5120, 4096], P('ep', 'tp', 'ctx'), may hold values from -0.3125 to 0.3125
- w_down: bfloat16 [2, 4096, 5120], P('ep', 'ctx', 'tp'), may hold values from -0.09375 to 0.09375
Outputs:
- layer_out: bfloat16 [4, 512, 5120], P(('groups', 'ep'), 'ctx', 'tp'), parts along dimension 0
There are 2 independent parts, one for each index of `groups`. A program takes and returns all parts, laid end to end along the dimension named above; an argument that names none is the same for every part. Nothing has to cross between parts.
Inputs may be any that keep to these rules, and one draw needn't show every extreme that they name: `expert_ids`: among the positions of one device, each expert below 2 is named at most 2 times; in every draw one of them is named exactly 2 times on every device.
All inputs are finite; a program needn't handle non-finite values.
Results may differ from a plain program's by a relative error of at most 0.023.
Values may be sent and summed in bfloat16 or wider, within the bound.
A program may use at most 64 MiB of HBM per device.

v0:
```python
import jax
import jax.numpy as jnp
from jax import lax
from jax.sharding import PartitionSpec as P

HEAD_WIDTH = 128
CAP = 2


def block_width(key_count):
    for candidate in (512, 256, 128):
        return candidate
    return key_count


def fresh_state(query_rows, kv_heads, group_width):
    return (
        jnp.full((kv_heads, group_width, query_rows), -1e30, jnp.float32),
        jnp.zeros((kv_heads, group_width, query_rows), jnp.float32),
        jnp.zeros((query_rows, kv_heads, group_width, HEAD_WIDTH), jnp.float32),
    )


def absorb_block(status, query_half, query_pos, key_block, value_block, key_pos):
    old_max, totals, weighted = status
    scores = jnp.einsum(
        "rgqd,kgd->gqrk", query_half, key_block, preferred_element_type=jnp.float32
    ) * HEAD_WIDTH ** (-0.5)
    visible = query_pos[:, None] >= key_pos[None, :]
    scores = jnp.where(visible, scores, -1e30)
    running_max = jnp.maximum(old_max, jnp.max(scores, axis=3))
    factor = jnp.exp(old_max - running_max)
    weights = jnp.where(visible, jnp.exp(scores - running_max[..., None]), 0.0)
    totals = totals * factor + jnp.sum(weights, axis=3)
    update = jnp.einsum(
        "gqrk,kgd->rgqd",
        weights.astype(jnp.bfloat16),
        value_block,
        preferred_element_type=jnp.float32,
    )
    weighted = weighted * jnp.transpose(factor, (2, 0, 1))[..., None] + update
    return (running_max, totals, weighted)


def finish(status, row_count):
    old_max, totals, weighted = status
    normed = weighted / jnp.transpose(totals, (2, 0, 1))[..., None]
    return normed.astype(jnp.bfloat16).reshape(row_count, -1)


def shards(queries, keys, values, expert_ids, router, w_gate, w_up, w_down):
    row_count = queries.shape[1]
    half_rows = row_count // 2
    feature_width = queries.shape[2]
    kv_heads = keys.shape[2] // HEAD_WIDTH
    group_width = feature_width // HEAD_WIDTH // kv_heads
    ep_count = lax.axis_size("ep")
    ctx_place = lax.axis_index("ctx")
    local_queries = queries[0].reshape(row_count, kv_heads, group_width, HEAD_WIDTH)
    lead_half = local_queries[:half_rows]
    tail_half = local_queries[half_rows:]
    lead_pos = ctx_place * row_count + jnp.arange(half_rows, dtype=jnp.int32)
    tail_pos = ctx_place * row_count + half_rows + jnp.arange(half_rows, dtype=jnp.int32)
    initial = (
        fresh_state(half_rows, kv_heads, group_width),
        fresh_state(half_rows, kv_heads, group_width),
    )
    key_piece = lax.all_gather(keys, "ctx", axis=1, tiled=True)[0]
    key_count = key_piece.shape[0]
    key_block_rows = block_width(key_count)
    block_count = key_count // key_block_rows
    key_blocks = key_piece.reshape(block_count, key_block_rows, kv_heads, HEAD_WIDTH)
    value_blocks = lax.all_gather(values, "ctx", axis=1, tiled=True)[0].reshape(
        block_count, key_block_rows, kv_heads, HEAD_WIDTH
    )
    offsets = jnp.arange(block_count, dtype=jnp.int32) * key_block_rows

    def one_block(status, inputs):
        key_block, value_block, block_begin = inputs
        key_pos = block_begin + jnp.arange(key_block_rows, dtype=jnp.int32)
        lead_state = lax.cond(
            block_begin <= lead_pos[-1],
            lambda kept_state: absorb_block(
                kept_state, lead_half, lead_pos, key_block, value_block, key_pos
            ),
            lambda kept_state: kept_state,
            status[0],
        )
        tail_state = lax.cond(
            block_begin <= tail_pos[-1],
            lambda kept_state: absorb_block(
                kept_state, tail_half, tail_pos, key_block, value_block, key_pos
            ),
            lambda kept_state: kept_state,
            status[1],
        )
        return ((lead_state, tail_state), None)

    result, _ = lax.scan(one_block, initial, (key_blocks, value_blocks, offsets))
    lead_status, tail_status = result
    lead_out = finish(lead_status, half_rows)
    tail_out = finish(tail_status, half_rows)
    attended = jnp.concatenate([lead_out, tail_out], axis=0)
    chosen = expert_ids[0, :, 0]
    choose = (chosen[:, None] == jnp.arange(ep_count, dtype=jnp.int32)[None, :]).astype(jnp.int32)
    earlier = jnp.cumsum(choose, axis=0) - choose
    slot_index = jnp.sum(earlier * choose, axis=1)
    target = chosen * CAP + slot_index
    spread = (target[None, :] == jnp.arange(ep_count * CAP, dtype=jnp.int32)[:, None]).astype(
        jnp.bfloat16
    )
    outgoing = jnp.dot(spread, attended, preferred_element_type=jnp.float32).astype(jnp.bfloat16)
    arrived = lax.all_to_all(
        outgoing.reshape(ep_count, CAP, feature_width),
        "ep",
        split_axis=0,
        concat_axis=0,
        tiled=True,
    )
    gathered = lax.all_gather(arrived[None], "ctx", axis=0, tiled=True)
    members = gathered.reshape(-1, feature_width)
    gate_w = w_gate[0]
    up_w = w_up[0]
    down_w = w_down[0]
    gate_part = jnp.dot(members, gate_w, preferred_element_type=jnp.float32)
    up_part = jnp.dot(members, up_w, preferred_element_type=jnp.float32)
    score_part = jnp.dot(members, router, preferred_element_type=jnp.float32)
    gate_sum, up_sum, router_score = (
        lax.psum(gate_part.astype(jnp.bfloat16), "tp").astype(jnp.float32),
        lax.psum(up_part.astype(jnp.bfloat16), "tp").astype(jnp.float32),
        lax.psum(score_part.astype(jnp.bfloat16), "tp").astype(jnp.float32),
    )
    weight = jax.nn.sigmoid(router_score)
    hidden = (jax.nn.silu(weight * gate_sum) * (weight * up_sum)).astype(jnp.bfloat16)
    expert_rows = lax.psum_scatter(
        jnp.dot(hidden, down_w, preferred_element_type=jnp.float32).astype(jnp.bfloat16),
        "ctx",
        scatter_dimension=0,
        tiled=True,
    )
    returned = lax.all_to_all(
        expert_rows.reshape(ep_count, CAP, feature_width),
        "ep",
        split_axis=0,
        concat_axis=0,
        tiled=True,
    )
    returned = returned.reshape(ep_count * CAP, feature_width)
    routed = lax.dot_general(
        spread, returned, (((0,), (0,)), ((), ())), preferred_element_type=jnp.float32
    )
    layer_out = (attended.astype(jnp.float32) + routed).astype(jnp.bfloat16)
    return layer_out[None]


def solution(mesh):
    placed = (
        P(("groups", "ep"), "ctx", "tp"),
        P(("groups", "ep"), "ctx", "tp"),
        P(("groups", "ep"), "ctx", "tp"),
        P(("groups", "ep"), "ctx", None),
        P("tp", "ep"),
        P("ep", "tp", "ctx"),
        P("ep", "tp", "ctx"),
        P("ep", "ctx", "tp"),
    )
    return jax.shard_map(
        shards,
        mesh=mesh,
        in_specs=placed,
        out_specs=P(("groups", "ep"), "ctx", "tp"),
        check_vma=False,
    )
```

profile of v0, /device:TPU:0, one launch (start us, length us, event | category | flops | bytes accessed | tf_op | source)
XLA Modules:
  0.0 157.5 jit_solution(6667889364840034550)
XLA Ops:
  6.5 1.0 copy.23
  7.6 16.7 %all_gather.9 = bf16[1,512,512]{1,2,0:T(8,128)(2,1)S(1)} all-gather(bf16[1,128,512]{1,2,0:T(8,128)(2,1)S(1)} %copy.23), channel_id=1, replica_groups=mesh['groups'=2,'ctx'=4,'ep'=2,'tp'=2] {'ctx'}, dimensions={1}, use_global_device_ids=true | all-gather | bytes 655360 | tf_op jit(solution)/shard_map/all_gather | solution.py:68
  24.3 1.0 copy.24
  25.3 14.6 %all_gather.10 = bf16[1,512,512]{1,2,0:T(8,128)(2,1)S(1)} all-gather(bf16[1,128,512]{1,2,0:T(8,128)(2,1)S(1)} %copy.24), channel_id=1, replica_groups=mesh['groups'=2,'ctx'=4,'ep'=2,'tp'=2] {'ctx'}, dimensions={1}, use_global_device_ids=true | all-gather | bytes 655360 | tf_op jit(solution)/shard_map/all_gather | solution.py:73
  39.9 0.6 slice.23
  41.2 0.6 broadcast.43
  41.8 4.8 %conditional.3 = (f32[4,5,64]{2,1,0:T(8,128)S(1)}, f32[64,4,5,128]{3,0,2,1:T(8,128)S(1)}) conditional(s32[]{:T(128)} %bitcast.14, (f32[4,5,64]{2,1,0:T(8,128)}, f32[64,4,5,128]{3,0,2,1:T(8,128)S(1)}) %tuple.31, (s32[64]{0:T(128)S(1)}, s32[512]{0:T(512)S(1)}, bf16[1,128,2560]{2,1,0:T(8,128)(2,1)}, bf16[512,4,128]{0,2,1:T(8,128)(2,1)S(1)}, ...), branch_computations={%region_4.5_spmd, %region_5.0_spmd} | conditional | flops 344428288 | bytes 12067088 | solution.py:89
  41.9 1.0 slice.18
  43.3 0.7 fusion.20
  44.0 0.9 fusion.22
  44.9 0.7 multiply_add_fusion.1
  45.6 1.1 fusion.29
  47.6 0.6 slice.22
  48.8 5.9 %conditional.2 = ((f32[4,5,64]{2,1,0:T(8,128)}, f32[64,4,5,128]{3,0,2,1:T(8,128)S(1)})) conditional(s32[]{:T(128)} %bitcast.10, (f32[4,5,64]{2,1,0:T(8,128)}, f32[64,4,5,128]{3,0,2,1:T(8,128)S(1)}) %tuple.31, (s32[64]{0:T(128)S(1)}, s32[512]{0:T(512)S(1)}, bf16[1,128,2560]{2,1,0:T(8,128)(2,1)S(1)}, bf16[512,4,128]{0,2,1:T(8,128)(2,1)S(1)}, ...), branch_computations={%region_0.1_spmd, %region_1.4_spmd} | conditional | flops 344428288 | bytes 12239212 | solution.py:81
  48.8 0.7 broadcast_compare_fusion
  50.0 1.4 fusion
  51.4 0.9 fusion.2
  52.3 1.3 multiply_add_fusion
  53.6 1.1 fusion.9
  54.7 1.0 divide_convert_fusion.1
  57.1 6.4 %all_to_all.10 = bf16[2,2,2560]{2,1,0:T(2,128)(2,1)S(1)} all-to-all(bf16[2,2,2560]{2,1,0:T(2,128)(2,1)S(1)} %reshape.58), channel_id=1, replica_groups=mesh['groups'=2,'ctx'=4,'ep'=2,'tp'=2] {'ep'}, dimensions={0} | all-to-all | bytes 40960 | tf_op jit(solution)/shard_map/all_to_all | solution.py:113
  63.5 13.2 %all-gather = bf16[8,2,2560]{2,1,0:T(2,128)(2,1)S(1)} all-gather(bf16[2,2,2560]{2,1,0:T(2,128)(2,1)S(1)} %all_to_all.10), channel_id=2, replica_groups=mesh['groups'=2,'ctx'=4,'ep'=2,'tp'=2] {'ctx'}, dimensions={0}, use_global_device_ids=true | all-gather | bytes 102400 | tf_op jit(solution)/shard_map/all_gather | solution.py:120
  76.7 3.9 %fusion.51 = bf16[16,1024]{1,0:T(8,128)(2,1)} fusion(bf16[16,2560]{1,0:T(8,128)(2,1)S(1)} %reshape.59, bf16[1,2560,1024]{2,1,0:T(8,128)(2,1)} %param.17), kind=kOutput, calls=%fused_computation.51 | convolution fusion | flops 83902464 | bytes 5357568 | tf_op jit(solution)/shard_map/dot_general | solution.py:125
  80.6 3.9 %fusion.54 = bf16[16,1024]{1,0:T(8,128)(2,1)} fusion(bf16[16,2560]{1,0:T(8,128)(2,1)S(1)} %reshape.59, bf16[1,2560,1024]{2,1,0:T(8,128)(2,1)} %param.18), kind=kOutput, calls=%fused_computation.52 | convolution fusion | flops 83902464 | bytes 5357568 | tf_op jit(solution)/shard_map/dot_general | solution.py:126
  84.6 0.6 fusion.58
  85.3 16.5 %all-reduce.7.cloned.1.call-done = (bf16[16,1024]{1,0:T(8,128)(2,1)}, bf16[16,1024]{1,0:T(8,128)(2,1)}, bf16[16,1]{0,1:T(2,128)(2,1)}) async-done(((bf16[16,1024]{1,0:T(8,128)(2,1)}, bf16[16,1024]{1,0:T(8,128)(2,1)}, bf16[16,1]{0,1:T(2,128)(2,1)}), (bf16[16,1024]{1,0:T(8,128)(2,1)}, bf16[16,1024]{1,0:T(8,128)(2,1)}, bf16[16,1]{0,1:T(2,128)(2,1)})) %all-reduce.7.cloned.1.call-update) | async-done | bytes 65584 | tf_op jit(solution)/shard_map/psum | solution.py:130
  101.8 0.7 divide_bitcast_fusion
  102.5 4.0 %fusion.48 = bf16[16,2560]{1,0:T(8,128)(2,1)} fusion(bf16[1,1024,2560]{2,1,0:T(8,128)(2,1)} %param.19, bf16[16,1024]{1,0:T(8,128)(2,1)} %get-tuple-element.178, bf16[16,1024]{1,0:T(8,128)(2,1)} %get-tuple-element.179, f32[16]{0:T(128)S(1)} %divide_bitcast_fusion), kind=kOutput, calls=%fused_computation.49 | convolution fusion | flops 84090880 | bytes 5390400 | tf_op jit(solution)/shard_map/dot_general | solution.py:136
  107.7 34.5 %all-reduce.5.cloned.1.call-done = bf16[16,2560]{1,0:T(8,128)(2,1)} async-done(((bf16[16,2560]{1,0:T(8,128)(2,1)}), bf16[16,2560]{1,0:T(8,128)(2,1)}) %all-reduce.5.cloned.1.call-update) | async-done | bytes 81936
  142.2 0.8 constant_dynamic-slice_fusion
  143.0 6.4 %all_to_all.11 = bf16[2,2,2560]{2,1,0:T(2,128)(2,1)S(1)} all-to-all(bf16[2,2,2560]{2,1,0:T(2,128)(2,1)S(1)} %reshape.61), channel_id=1, replica_groups=mesh['groups'=2,'ctx'=4,'ep'=2,'tp'=2] {'ep'}, dimensions={0} | all-to-all | bytes 40960 | tf_op jit(solution)/shard_map/all_to_all | solution.py:141
  149.5 1.2 fusion.47
  (47 shorter events, 3.9 us)
Async XLA Ops:
  6.5 78.0 %copy-start = (bf16[2560,1]{0,1:T(2,128)(2,1)S(1)}, bf16[2560,1]{0,1:T(2,128)(2,1)}, u32[]{:S(2)}) copy-start(bf16[2560,1]{0,1:T(2,128)(2,1)} %param.16) | copy-start | bytes 15364
  6.5 95.3 %all-reduce.7.cloned.1.call-start = ((), (), s32[]{:S(2)}) async-start(), calls=%async_computation.3 | async-start | bytes 132096 | tf_op jit(solution)/shard_map/psum | solution.py:130
  46.7 2.1 %copy-start.1 = (bf16[1,128,2560]{2,1,0:T(8,128)(2,1)S(1)}, bf16[1,128,2560]{2,1,0:T(8,128)(2,1)}, u32[]{:S(2)}) copy-start(bf16[1,128,2560]{2,1,0:T(8,128)(2,1)} %param.12) | copy-start | bytes 1966084
  48.8 0.7 copy-start.2
  49.6 1.8 %copy-start.3 = (f32[4,5,64]{2,1,0:T(8,128)S(1)}, f32[4,5,64]{2,1,0:T(8,128)}, u32[]{:S(2)}) copy-start(f32[4,5,64]{2,1,0:T(8,128)} %copy-done.2) | copy-start | bytes 15364 | tf_op jit(solution)/shard_map/while/body/eval_jaxpr/cond
  49.6 1.9 %copy-start.4 = (pred[64,512]{1,0:T(8,128)(4,1)S(1)}, pred[64,512]{1,0:T(8,128)(4,1)}, u32[]{:S(2)}) copy-start(pred[64,512]{1,0:T(8,128)(4,1)} %broadcast_compare_fusion) | copy-start | bytes 98308 | tf_op jit(solution)/shard_map/while/body/eval_jaxpr/cond
  54.7 1.6 %copy-start.5 = (s32[1,128,1]{1,2,0:T(1,128)S(1)}, s32[1,128,1]{1,2,0:T(1,128)}, u32[]{:S(2)}) copy-start(s32[1,128,1]{1,2,0:T(1,128)} %param.15) | copy-start | bytes 1540
  85.2 57.0 %all-reduce.5.cloned.1.call-start = ((), (), s32[]{:S(2)}) async-start(), calls=%async_computation.2 | async-start | bytes 163840
  102.5 4.1 %copy-start.6 = (u32[32]{0:T(128)S(1)}, u32[32]{0:T(128)}, u32[]{:S(2)}) copy-start(u32[32]{0:T(128)} %constant.73) | copy-start | bytes 388
Sparse Core Ops, SparseCore 0:
  85.3 16.4 all-reduce.6
  106.7 35.4 all-reduce.4
where the time goes:
time: 158 us
  blocking collectives  57.4 us (36%)
  waiting for transfers between devices  51.1 us (32%)
  matrix products  18.1 us (11%)
  between operations  15.5 us (10%)
  local copies, waits for them, and re-layouts  8.44 us (5%)
  other arithmetic  6.94 us (4%)
    unnamed x3, waiting for transfers between devices  34.5 us
    all_gather x1, blocking collectives, shards(): key_piece = lax.all_gather(keys, 'ctx', axis=1, tiled=True)[0]  16.7 us
    psum x1, waiting for transfers between devices, shards(): lax.psum(up_part.astype(jnp.bfloat16), 'tp').astype(jnp.float32)  16.5 us
    all_gather x1, blocking collectives, shards(): lax.all_gather(values, 'ctx', axis=1, tiled=True)[0]  14.6 us
    all_gather x1, blocking collectives, shards(): gathered = lax.all_gather(arrived[None], 'ctx', axis=0, tiled=True)  13.2 us
    all_to_all x1, blocking collectives, shards(): lax.all_to_all(outgoing.reshape(ep_count, CAP, feature_width), 'ep', spli...  6.44 us
    all_to_all x1, blocking collectives, shards(): lax.all_to_all(expert_rows.reshape(ep_count, CAP, feature_width), 'ep', s...  6.41 us
    dot_general x1, matrix products, shards(): jnp.dot(hidden, down_w, preferred_element_type=jnp.float32)  4.03 us
  transfers between devices with their start and end apart: 2, of which 2 were waited for; matrix products, arithmetic and copies ran while one was open for 0% of the time, Pallas kernels for 0%

commit v1 on v0

--- a/solution.py
+++ b/solution.py
@@ -65,7 +65,7 @@
         fresh_state(half_rows, kv_heads, group_width),
         fresh_state(half_rows, kv_heads, group_width),
     )
-    key_piece = lax.all_gather(keys, "ctx", axis=1, tiled=True)[0]
+    key_piece = jnp.concatenate(lax.all_gather(keys, "ctx"), axis=1)[0]
     key_count = key_piece.shape[0]
     key_block_rows = block_width(key_count)
     block_count = key_count // key_block_rows

time: 158 us -> 154 us (0.975)
  other arithmetic: 6.94 us -> 3.48 us
  local copies, waits for them, and re-layouts: 8.44 us -> 5.97 us
    add x2, other arithmetic: 2.06 us -> 0.03 us  [absorb_block(): totals = totals * factor + jnp.sum(weights, axis=3)]
    unnamed x13 -> x12, local copies, waits for them, and re-layouts: 3.45 us -> 2.45 us
where the time goes in v1:
time: 154 us
  blocking collectives  58.8 us (38%)
  waiting for transfers between devices  52.1 us (34%)
  matrix products  17.5 us (11%)
  between operations  15.5 us (10%)
  local copies, waits for them, and re-layouts  5.97 us (4%)
  other arithmetic  3.48 us (2%)
    unnamed x3, waiting for transfers between devices  34.5 us
    all_gather x1, blocking collectives, shards(): key_piece = jnp.concatenate(lax.all_gather(keys, 'ctx'), axis=1)[0]  17.7 us
    psum x1, waiting for transfers between devices, shards(): lax.psum(up_part.astype(jnp.bfloat16), 'tp').astype(jnp.float32)  17.6 us
    all_gather x1, blocking collectives, shards(): lax.all_gather(values, 'ctx', axis=1, tiled=True)[0]  15.1 us
    all_gather x1, blocking collectives, shards(): gathered = lax.all_gather(arrived[None], 'ctx', axis=0, tiled=True)  13.2 us
    all_to_all x1, blocking collectives, shards(): lax.all_to_all(outgoing.reshape(ep_count, CAP, feature_width), 'ep', spli...  6.43 us
    all_to_all x1, blocking collectives, shards(): lax.all_to_all(expert_rows.reshape(ep_count, CAP, feature_width), 'ep', s...  6.41 us
    dot_general x1, matrix products, shards(): jnp.dot(hidden, down_w, preferred_element_type=jnp.float32)  4.03 us
  transfers between devices with their start and end apart: 2, of which 2 were waited for; matrix products, arithmetic and copies ran while one was open for 0% of the time, Pallas kernels for 0%

profile of v1, /device:TPU:0, one launch (start us, length us, event | category | flops | bytes accessed | tf_op | source)
XLA Modules:
  0.0 153.6 jit_solution(426991621969007780)
XLA Ops:
  6.6 17.7 %all-gather = bf16[4,128,512]{2,1,0:T(8,128)(2,1)S(1)} all-gather(bf16[1,128,512]{2,1,0:T(8,128)(2,1)} %param.13), channel_id=2, replica_groups=mesh['groups'=2,'ctx'=4,'ep'=2,'tp'=2] {'ctx'}, dimensions={0}, use_global_device_ids=true | all-gather | bytes 655360 | tf_op jit(solution)/shard_map/all_gather | solution.py:68
  24.4 1.0 copy.22
  25.4 15.1 %all_gather.14 = bf16[1,512,512]{1,2,0:T(8,128)(2,1)S(1)} all-gather(bf16[1,128,512]{1,2,0:T(8,128)(2,1)S(1)} %copy.22), channel_id=1, replica_groups=mesh['groups'=2,'ctx'=4,'ep'=2,'tp'=2] {'ctx'}, dimensions={1}, use_global_device_ids=true | all-gather | bytes 655360 | tf_op jit(solution)/shard_map/all_gather | solution.py:73
  40.5 0.6 slice.23
  41.8 3.2 %conditional.3 = (f32[4,5,64]{2,1,0:T(8,128)S(1)}, f32[64,4,5,128]{3,0,2,1:T(8,128)S(1)}) conditional(s32[]{:T(128)} %bitcast.13, (f32[4,5,64]{2,1,0:T(8,128)S(1)}, f32[64,4,5,128]{3,0,2,1:T(8,128)S(1)}) %tuple.31, (s32[64]{0:T(128)S(1)}, s32[512]{0:T(512)S(1)}, bf16[1,128,2560]{2,1,0:T(8,128)(2,1)S(1)}, bf16[512,4,128]{2,1,0:T(4,128)(2,1)S(1)}, ...), branch_computations={%region_4.5_spmd, %region_5.0_spmd} | conditional | flops 344428288 | bytes 12067088 | solution.py:89
  42.0 0.4 slice.19
  42.4 0.7 fusion.20
  43.1 0.9 fusion.22
  44.0 1.1 fusion.29
  45.1 0.2 divide_convert_fusion
  45.6 0.4 reshape.57
  45.9 0.6 slice.22
  47.2 3.2 %conditional.2 = ((f32[4,5,64]{2,1,0:T(8,128)S(1)}, f32[64,4,5,128]{3,0,2,1:T(8,128)S(1)})) conditional(s32[]{:T(128)} %bitcast.10, (f32[4,5,64]{2,1,0:T(8,128)S(1)}, f32[64,4,5,128]{3,0,2,1:T(8,128)S(1)}) %tuple.31, (s32[64]{0:T(128)S(1)}, s32[512]{0:T(512)S(1)}, bf16[1,128,2560]{2,1,0:T(8,128)(2,1)S(1)}, bf16[512,4,128]{2,1,0:T(4,128)(2,1)S(1)}, ...), branch_computations={%region_0.1_spmd, %region_1.4_spmd} | conditional | flops 344428288 | bytes 12067096 | solution.py:81
  47.3 0.4 slice.17
  47.7 0.7 fusion
  48.5 0.9 fusion.2
  49.3 1.1 fusion.9
  50.4 0.2 divide_convert_fusion.1
  50.9 0.4 reshape.56
  52.0 6.4 %all_to_all.10 = bf16[2,2,2560]{2,1,0:T(2,128)(2,1)S(1)} all-to-all(bf16[2,2,2560]{2,1,0:T(2,128)(2,1)S(1)} %reshape.58), channel_id=1, replica_groups=mesh['groups'=2,'ctx'=4,'ep'=2,'tp'=2] {'ep'}, dimensions={0} | all-to-all | bytes 40960 | tf_op jit(solution)/shard_map/all_to_all | solution.py:113
  58.5 13.2 %all-gather.1 = bf16[8,2,2560]{2,1,0:T(2,128)(2,1)S(1)} all-gather(bf16[2,2,2560]{2,1,0:T(2,128)(2,1)S(1)} %all_to_all.10), channel_id=3, replica_groups=mesh['groups'=2,'ctx'=4,'ep'=2,'tp'=2] {'ctx'}, dimensions={0}, use_global_device_ids=true | all-gather | bytes 102400 | tf_op jit(solution)/shard_map/all_gather | solution.py:120
  71.7 3.9 %fusion.51 = bf16[16,1024]{1,0:T(8,128)(2,1)} fusion(bf16[16,2560]{1,0:T(8,128)(2,1)S(1)} %reshape.59, bf16[1,2560,1024]{2,1,0:T(8,128)(2,1)} %param.17), kind=kOutput, calls=%fused_computation.51 | convolution fusion | flops 83902464 | bytes 5357568 | tf_op jit(solution)/shard_map/dot_general | solution.py:125
  75.6 3.9 %fusion.54 = bf16[16,1024]{1,0:T(8,128)(2,1)} fusion(bf16[16,2560]{1,0:T(8,128)(2,1)S(1)} %reshape.59, bf16[1,2560,1024]{2,1,0:T(8,128)(2,1)} %param.18), kind=kOutput, calls=%fused_computation.52 | convolution fusion | flops 83902464 | bytes 5357568 | tf_op jit(solution)/shard_map/dot_general | solution.py:126
  79.5 0.7 fusion.58
  80.3 17.6 %all-reduce.7.cloned.1.call-done = (bf16[16,1024]{1,0:T(8,128)(2,1)}, bf16[16,1024]{1,0:T(8,128)(2,1)}, bf16[16,1]{0,1:T(2,128)(2,1)}) async-done(((bf16[16,1024]{1,0:T(8,128)(2,1)}, bf16[16,1024]{1,0:T(8,128)(2,1)}, bf16[16,1]{0,1:T(2,128)(2,1)}), (bf16[16,1024]{1,0:T(8,128)(2,1)}, bf16[16,1024]{1,0:T(8,128)(2,1)}, bf16[16,1]{0,1:T(2,128)(2,1)})) %all-reduce.7.cloned.1.call-update) | async-done | bytes 65584 | tf_op jit(solution)/shard_map/psum | solution.py:130
  97.9 0.6 divide_bitcast_fusion
  98.5 4.0 %fusion.48 = bf16[16,2560]{1,0:T(8,128)(2,1)} fusion(bf16[1,1024,2560]{2,1,0:T(8,128)(2,1)} %param.19, bf16[16,1024]{1,0:T(8,128)(2,1)} %get-tuple-element.178, bf16[16,1024]{1,0:T(8,128)(2,1)} %get-tuple-element.179, f32[16]{0:T(128)S(1)} %divide_bitcast_fusion), kind=kOutput, calls=%fused_computation.49 | convolution fusion | flops 84090880 | bytes 5390400 | tf_op jit(solution)/shard_map/dot_general | solution.py:136
  102.6 0.6 dynamic-slice
  103.8 34.4 %all-reduce.5.cloned.1.call-done = bf16[16,2560]{1,0:T(8,128)(2,1)} async-done(((bf16[16,2560]{1,0:T(8,128)(2,1)}), bf16[16,2560]{1,0:T(8,128)(2,1)}) %all-reduce.5.cloned.1.call-update) | async-done | bytes 81936
  138.2 0.8 constant_dynamic-slice_fusion
  139.0 6.4 %all_to_all.11 = bf16[2,2,2560]{2,1,0:T(2,128)(2,1)S(1)} all-to-all(bf16[2,2,2560]{2,1,0:T(2,128)(2,1)S(1)} %reshape.61), channel_id=1, replica_groups=mesh['groups'=2,'ctx'=4,'ep'=2,'tp'=2] {'ep'}, dimensions={0} | all-to-all | bytes 40960 | tf_op jit(solution)/shard_map/all_to_all | solution.py:141
  145.5 1.2 fusion.47
  (41 shorter events, 1.8 us)
Async XLA Ops:
  6.5 73.0 %copy-start = (bf16[2560,1]{0,1:T(2,128)(2,1)S(1)}, bf16[2560,1]{0,1:T(2,128)(2,1)}, u32[]{:S(2)}) copy-start(bf16[2560,1]{0,1:T(2,128)(2,1)} %param.16) | copy-start | bytes 15364
  6.5 35.3 %copy-start.1 = (bf16[1,128,2560]{2,1,0:T(8,128)(2,1)S(1)}, bf16[1,128,2560]{2,1,0:T(8,128)(2,1)}, u32[]{:S(2)}) copy-start(bf16[1,128,2560]{2,1,0:T(8,128)(2,1)} %param.12) | copy-start | bytes 1966084
  6.5 91.4 %all-reduce.7.cloned.1.call-start = ((), (), s32[]{:S(2)}) async-start(), calls=%async_computation.3 | async-start | bytes 132096 | tf_op jit(solution)/shard_map/psum | solution.py:130
  50.4 0.9 copy-start.2
  80.2 58.0 %all-reduce.5.cloned.1.call-start = ((), (), s32[]{:S(2)}) async-start(), calls=%async_computation.2 | async-start | bytes 163840
  98.5 4.1 %copy-start.3 = (u32[32]{0:T(128)S(1)}, u32[32]{0:T(128)}, u32[]{:S(2)}) copy-start(u32[32]{0:T(128)} %constant.73) | copy-start | bytes 388
Sparse Core Ops, SparseCore 0:
  80.4 17.4 all-reduce.6
  102.7 35.4 all-reduce.4
